TPU v7x, 32 devices: a whole 2x2x4 slice. The times are simulated.
32 devices in a mesh: row: 16 (over z, y, core), head: 2 (over x).
Axes of the slice: x: 2, y: 2, z: 4, core: 2. Of those that a mesh axis runs over, the one named last changes fastest.
Arguments:
- pair_input: bfloat16 [32, 32, 128], P(('row', 'head')), may hold values from -6 to 6
- cotangent: bfloat16 [32, 32, 128], P(('row', 'head')), may hold values from -6 to 6
- residue_mask: int32 [32], replicated, may hold values from 0 to 1, as said below
- norm_gain: float32 [2, 128], replicated, may hold values from 0.5 to 1.5
- norm_shift: float32 [2, 128], replicated, may hold values from -3 to 3
- proj_weights: bfloat16 [2, 4, 128, 128], replicated, may hold values from -0.5 to 0.5
- gate_bias: float32 [2, 128], replicated, may hold values from -4 to 4
- out_weights: bfloat16 [2, 128, 128], replicated, may hold values from -1.0546875 to 1.0546875
- bias_weights: bfloat16 [2, 128, 4], replicated, may hold values from -1.06066017 to 1.06066017
Outputs:
- pair_grad: float32 [32, 32, 128], P(('row', 'head'))
- proj_grad: float32 [2, 4, 128, 128], replicated
- gate_bias_grad: float32 [2, 128], replicated
- out_grad: float32 [2, 128, 128], replicated
- bias_weight_grad: float32 [2, 128, 4], replicated
- gain_grad: float32 [2, 128], replicated
- shift_grad: float32 [2, 128], replicated
Inputs may be any that keep to these rules, and one draw needn't show every extreme that they name: `residue_mask`: 1 for the first residues of the crop and 0 for the padding after them; at least half of the 32 residues are 1.
All inputs are finite; a program needn't handle non-finite values.
Results may differ from a plain program's by a relative error of at most 0.02.
The roundings to bfloat16 on the way count: a program that leaves them out, or rounds other values in their place, can miss the bound.
Values may be sent and summed in bfloat16 or wider, within the bound.
A program may use at most 64 MiB of HBM per device.

v0:
```python
import functools
import math

import jax
import jax.numpy as jnp
from jax import lax
from jax.experimental import pallas as pl
from jax.experimental.pallas import tpu as pltpu
from jax.sharding import PartitionSpec as P

EPS = 1e-05
MASKED = 1000000000.0


def layer_norm(values, norm_scale, norm_offset):
    floats = values.astype(jnp.float32)
    centred = floats - jnp.mean(floats, axis=-1, keepdims=True)
    inverse = lax.rsqrt(jnp.mean(centred * centred, axis=-1, keepdims=True) + EPS)
    normed = centred * inverse
    return (normed, inverse, (normed * norm_scale + norm_offset).astype(jnp.bfloat16))


def norm_backward(grad_normal, normed, inverse, norm_scale):
    grad_hat = grad_normal * norm_scale
    first_mean = jnp.mean(grad_hat, axis=-1, keepdims=True)
    second_mean = jnp.mean(grad_hat * normed, axis=-1, keepdims=True)
    return inverse * (grad_hat - first_mean - normed * second_mean)


def class_columns(values, head_index, row_count, head_count, slab_rows):
    leading = values.shape[0]
    shaped = values.reshape(leading, row_count, head_count, slab_rows, values.shape[-1])
    picked = lax.dynamic_index_in_dim(shaped, head_index, axis=2, keepdims=False)
    return picked.reshape(leading, row_count * slab_rows, values.shape[-1])


def forward_block(pair_rows, key_bias, params, layout):
    norm_scale, norm_offset, projection, gate_offset, out_proj, bias_proj = params
    slab_rows, row_count, head_count, head_index = layout
    head_total = bias_proj.shape[1]
    inner_width = projection.shape[2]
    head_size = inner_width // head_total
    query_scale = 1.0 / math.sqrt(head_size)
    normed, inverse, normal_own = layer_norm(pair_rows, norm_scale, norm_offset)
    normal_rows = lax.all_gather(normal_own, "head", axis=0, tiled=True)
    bias_own = jnp.einsum(
        "snc,ch->hsn", normal_own, bias_proj, preferred_element_type=jnp.float32
    ).astype(jnp.bfloat16)
    bias_query = lax.all_gather(bias_own, "row", axis=1, tiled=True)
    normal_query = class_columns(normal_rows, head_index, row_count, head_count, slab_rows)
    block_rows = normal_query.shape[0]
    query_count = normal_query.shape[1]
    key_count = normal_rows.shape[1]
    queries = (
        jnp.dot(normal_query, projection[0], preferred_element_type=jnp.float32) * query_scale
    ).astype(jnp.bfloat16)
    joined_weights = jnp.concatenate([projection[1], projection[2]], axis=1)
    key_value = jnp.dot(normal_rows, joined_weights, preferred_element_type=jnp.float32).astype(
        jnp.bfloat16
    )
    gate_values = jax.nn.sigmoid(
        jnp.dot(normal_query, projection[3], preferred_element_type=jnp.float32) + gate_offset
    )
    head_queries = queries.reshape(block_rows, query_count, head_total, head_size).transpose(
        2, 0, 1, 3
    )
    head_pairs = key_value.reshape(block_rows, key_count, 2, head_total, head_size).transpose(
        2, 3, 0, 1, 4
    )

    def attend(inputs):
        query_head, key_head, value_head, bias_head = inputs
        logits = jnp.einsum(
            "rqd,rnd->rqn", query_head, key_head, preferred_element_type=jnp.float32
        )
        logits = logits + bias_head.astype(jnp.float32)[None] + key_bias
        largest = jnp.max(logits, axis=-1, keepdims=True)
        weights = jnp.exp(logits - largest)
        total = jnp.sum(weights, axis=-1, keepdims=True)
        soft_weights = weights / total
        attended = jnp.einsum(
            "rqn,rnd->rqd",
            soft_weights.astype(jnp.bfloat16),
            value_head,
            preferred_element_type=jnp.float32,
        )
        return ((largest + jnp.log(total))[..., 0], attended)

    log_totals, attended = lax.map(attend, (head_queries, head_pairs[0], head_pairs[1], bias_query))
    attended = attended.transpose(1, 2, 0, 3).reshape(block_rows, query_count, inner_width)
    gated_out = (gate_values * attended).astype(jnp.bfloat16)
    update = jnp.dot(gated_out, out_proj, preferred_element_type=jnp.float32).astype(jnp.bfloat16)
    saved_state = (
        normed,
        inverse,
        normal_own,
        normal_rows,
        normal_query,
        head_queries,
        head_pairs,
        bias_query,
        gate_values,
        attended,
        gated_out,
        log_totals,
    )
    return (saved_state, update)


def backward_block(saved_state, grad_query, key_bias, params, layout):
    norm_scale, norm_offset, projection, gate_offset, out_proj, bias_proj = params
    slab_rows, row_count, head_count, head_index = layout
    (
        normed,
        inverse,
        normal_own,
        normal_rows,
        normal_query,
        head_queries,
        head_pairs,
        bias_query,
        gate_values,
        attended,
        gated_out,
        log_totals,
    ) = saved_state
    channels = normal_own.shape[2]
    head_total, block_rows, query_count, head_size = head_queries.shape
    key_count = normal_rows.shape[1]
    inner_width = head_total * head_size
    query_scale = 1.0 / math.sqrt(head_size)
    grad_gated = jnp.dot(grad_query, out_proj.T, preferred_element_type=jnp.float32)
    grad_att = (grad_gated * gate_values).astype(jnp.bfloat16)
    grad_pre = (grad_gated * attended * gate_values * (1.0 - gate_values)).astype(jnp.bfloat16)
    head_grads = grad_att.reshape(block_rows, query_count, head_total, head_size).transpose(
        2, 0, 1, 3
    )

    def differentiate(inputs):
        total_head, query_head, key_head, value_head, bias_head, grad_head = inputs
        logits = jnp.einsum(
            "rqd,rnd->rqn", query_head, key_head, preferred_element_type=jnp.float32
        )
        logits = logits + bias_head.astype(jnp.float32)[None] + key_bias
        soft_weights = jnp.exp(logits - total_head[..., None])
        grad_weights = jnp.einsum(
            "rqd,rnd->rqn", grad_head, value_head, preferred_element_type=jnp.float32
        )
        grad_logits = soft_weights * (
            grad_weights - jnp.sum(soft_weights * grad_weights, axis=-1, keepdims=True)
        )
        logits_half = grad_logits.astype(jnp.bfloat16)
        grad_queries = (
            jnp.einsum("rqn,rnd->rqd", logits_half, key_head, preferred_element_type=jnp.float32)
            * query_scale
        ).astype(jnp.bfloat16)
        grad_keys = jnp.einsum(
            "rqn,rqd->rnd", logits_half, query_head, preferred_element_type=jnp.float32
        ).astype(jnp.bfloat16)
        grad_values = jnp.einsum(
            "rqn,rqd->rnd",
            soft_weights.astype(jnp.bfloat16),
            grad_head,
            preferred_element_type=jnp.float32,
        ).astype(jnp.bfloat16)
        return (grad_queries, grad_keys, grad_values, jnp.sum(grad_logits, axis=0))

    grad_queries, grad_keys, grad_values, grad_bias = lax.map(
        differentiate,
        (log_totals, head_queries, head_pairs[0], head_pairs[1], bias_query, head_grads),
    )
    grad_queries = grad_queries.transpose(1, 2, 0, 3).reshape(block_rows, query_count, inner_width)
    key_weights = projection[1].reshape(channels, head_total, head_size).transpose(1, 2, 0)
    value_weights = projection[2].reshape(channels, head_total, head_size).transpose(1, 2, 0)
    query_side = jnp.dot(grad_queries, projection[0].T, preferred_element_type=jnp.float32)
    query_side = query_side + jnp.dot(grad_pre, projection[3].T, preferred_element_type=jnp.float32)
    count = slab_rows * lax.axis_size("head")
    term = jnp.einsum("hrnd,hdc->rnc", grad_keys, key_weights, preferred_element_type=jnp.float32)
    term = term + jnp.einsum(
        "hrnd,hdc->rnc", grad_values, value_weights, preferred_element_type=jnp.float32
    )
    shaped = term.reshape(count, row_count, head_count, slab_rows, channels)
    current = lax.dynamic_slice_in_dim(shaped, head_index, 1, 2)
    query_slice = query_side.reshape(count, row_count, 1, slab_rows, channels)
    shaped = lax.dynamic_update_slice_in_dim(shaped, current + query_slice, head_index, 2)
    grad_normal = lax.psum_scatter(
        shaped.reshape(count, key_count, channels).astype(jnp.bfloat16),
        "head",
        scatter_dimension=0,
        tiled=True,
    ).astype(jnp.float32)
    bias_total = lax.psum_scatter(grad_bias, "row", scatter_dimension=1, tiled=True)
    bias_half = bias_total.astype(jnp.bfloat16)
    grad_normal = grad_normal + jnp.einsum(
        "hsn,ch->snc", bias_half, bias_proj, preferred_element_type=jnp.float32
    )
    grad_pair = norm_backward(grad_normal, normed, inverse, norm_scale)
    projection_grads = jnp.stack(
        [
            jnp.einsum(
                "rqc,rqe->ce", normal_query, grad_queries, preferred_element_type=jnp.float32
            ),
            jnp.einsum(
                "rnc,hrnd->chd", normal_rows, grad_keys, preferred_element_type=jnp.float32
            ).reshape(channels, inner_width),
            jnp.einsum(
                "rnc,hrnd->chd", normal_rows, grad_values, preferred_element_type=jnp.float32
            ).reshape(channels, inner_width),
            jnp.einsum("rqc,rqe->ce", normal_query, grad_pre, preferred_element_type=jnp.float32),
        ]
    )
    weight_grads = (
        projection_grads,
        jnp.sum(grad_pre.astype(jnp.float32), axis=(0, 1)),
        jnp.einsum("rqe,rqc->ec", gated_out, grad_query, preferred_element_type=jnp.float32),
        jnp.einsum("snc,hsn->ch", normal_own, bias_half, preferred_element_type=jnp.float32),
        jnp.sum(grad_normal * normed, axis=(0, 1)),
        jnp.sum(grad_normal, axis=(0, 1)),
    )
    return (grad_pair, weight_grads)


def to_queries(grad_rows, layout):
    slab_rows, row_count, head_count, head_index = layout
    channels = grad_rows.shape[2]
    shaped = grad_rows.reshape(slab_rows, row_count, head_count, slab_rows, channels)
    moved = lax.all_to_all(shaped, "head", split_axis=2, concat_axis=0, tiled=True)
    return moved.reshape(slab_rows * head_count, row_count * slab_rows, channels)


def sum_side(weight_grads):
    return lax.psum(
        (
            weight_grads[0],
            weight_grads[1],
            weight_grads[2],
            weight_grads[3],
            weight_grads[4],
            weight_grads[5],
        ),
        ("row", "head"),
    )


def local(
    pair_input,
    cotangent,
    residue_mask,
    norm_gain,
    norm_shift,
    proj_weights,
    gate_bias,
    out_weights,
    bias_weights,
):
    slab_rows = pair_input.shape[0]
    channels = pair_input.shape[2]
    row_count = lax.axis_size("row")
    head_count = lax.axis_size("head")
    layout = (slab_rows, row_count, head_count, lax.axis_index("head"))
    key_bias = (residue_mask.astype(jnp.float32) - 1.0) * MASKED
    params = [
        (
            norm_gain[which],
            norm_shift[which],
            proj_weights[which],
            gate_bias[which],
            out_weights[which],
            bias_weights[which],
        )
        for which in range(2)
    ]
    first_state, first_update = forward_block(pair_input, key_bias, params[0], layout)
    returned = lax.all_to_all(
        first_update.reshape(slab_rows * head_count, row_count, 1, slab_rows, channels),
        "head",
        split_axis=0,
        concat_axis=2,
        tiled=True,
    )
    after_first = (
        pair_input.astype(jnp.float32)
        + returned.reshape(slab_rows, -1, channels).astype(jnp.float32)
    ).astype(jnp.bfloat16)
    joined = jnp.concatenate([after_first, cotangent], axis=2)
    moved = lax.all_to_all(
        lax.all_to_all(
            joined.reshape(1, 1, slab_rows, row_count, head_count, slab_rows, 2 * channels),
            "row",
            split_axis=3,
            concat_axis=0,
            tiled=True,
        ),
        "head",
        split_axis=4,
        concat_axis=1,
        tiled=True,
    )
    flipped = moved.reshape(-1, slab_rows, 2 * channels).transpose(1, 0, 2)
    second_state, second_update = forward_block(
        flipped[:, :, :channels], key_bias, params[1], layout
    )
    second_grad, second_weights = backward_block(
        second_state, to_queries(flipped[:, :, channels:], layout), key_bias, params[1], layout
    )
    second_weights = sum_side(second_weights)
    sent_back = lax.all_to_all(
        lax.all_to_all(
            second_grad.astype(jnp.bfloat16).reshape(
                1, 1, slab_rows, row_count, head_count, slab_rows, channels
            ),
            "row",
            split_axis=3,
            concat_axis=0,
            tiled=True,
        ),
        "head",
        split_axis=4,
        concat_axis=1,
        tiled=True,
    )
    end_grad = sent_back.reshape(-1, slab_rows, channels).transpose(1, 0, 2)
    grad_after = cotangent.astype(jnp.float32) + end_grad.astype(jnp.float32)
    start_grad, first_weights = backward_block(
        first_state,
        to_queries(grad_after.astype(jnp.bfloat16), layout),
        key_bias,
        params[0],
        layout,
    )
    pair_grad = grad_after + start_grad
    first_weights = sum_side(first_weights)
    stacked = [
        jnp.stack([start_part, end_part])
        for start_part, end_part in zip(first_weights, second_weights)
    ]
    return (pair_grad, stacked[0], stacked[1], stacked[2], stacked[3], stacked[4], stacked[5])


MESH = pl.DeviceIdType.MESH
F32 = jnp.float32
BF16 = jnp.bfloat16
TILE = 16
RESIDENT = 4
NN = ((1,), (0,))
NT = ((1,), (1,))
TN = ((0,), (0,))


def mm(a, b, contract):
    return lax.dot_general(a, b, (contract, ((), ())), preferred_element_type=F32)


def fused_kernel(
    n_head,
    held,
    group,
    heads,
    pair_ref,
    cot_ref,
    mask_ref,
    gain_ref,
    shift_ref,
    proj_far,
    gate_ref,
    out_far,
    bias_ref,
    pair_out,
    weights_out,
    small_out,
    stage_in,
    got_in,
    stage_bias,
    got_bias,
    stage_flip,
    got_flip,
    stage_bias1,
    got_bias1,
    stage_back,
    got_back,
    stage_sum,
    got_sum,
    stage_w,
    got_w,
    own_w,
    all_w,
    stage_small,
    got_small,
    result,
    proj_ref,
    out_ref,
    send_sem,
    recv_sem,
    load_sem,
):
    loads = [
        pltpu.make_async_copy(far, near, load_sem.at[i])
        for i, (far, near) in enumerate(((proj_far, proj_ref), (out_far, out_ref)))
    ]
    for load in loads:
        load.start()
    me = lax.axis_index("row") * n_head + lax.axis_index("head")
    layer = me // group
    seat = me % group
    nres, channels = pair_ref.shape[1:]
    inner = proj_ref.shape[3]
    hdim = inner // heads
    wide = heads * nres
    cells = held * nres
    scale = 1.0 / math.sqrt(hdim)
    barrier = pltpu.get_barrier_semaphore()
    waits = []

    def coords(device):
        return (device // n_head, device % n_head)

    def each_mate(action):
        def step(offset, carry):
            other = lax.rem(seat + offset, group)
            action(other, coords(layer * group + other))
            return carry

        lax.fori_loop(1, group, step, 0)

    def each_twin(action):
        def step(offset, carry):
            other = lax.rem(layer + offset, held)
            action(other, coords(other * group + seat))
            return carry

        lax.fori_loop(1, held, step, 0)

    def each_other(action):
        def step(offset, carry):
            other = lax.rem(me + offset, group * held)
            action(other, coords(other))
            return carry

        lax.fori_loop(1, group * held, step, 0)

    def send(source_of, target, channel, each=each_mate, slot=None):
        place = seat if slot is None else slot

        def start(other, device):
            pltpu.make_async_remote_copy(
                src_ref=source_of(other),
                dst_ref=target.at[place],
                send_sem=send_sem.at[channel],
                recv_sem=recv_sem.at[channel],
                device_id=device,
                device_id_type=MESH,
            ).start()

        each(start)
        waits.append((target, channel))

    def wait_all(target, sem):
        view = target.at[pl.ds(0, target.shape[0] - 1)]
        pltpu.make_async_copy(view, view, sem).wait()

    def received(target, channel):
        wait_all(target, recv_sem.at[channel])

    def greet(other, device):
        pl.semaphore_signal(barrier, inc=1, device_id=device, device_id_type=MESH)

    each_other(greet)

    def iota(shape, dim):
        return lax.broadcasted_iota(jnp.int32, shape, dim)

    def natural(position):
        return position % held * group + position // held

    head_mask = (iota((wide, inner), 0) // nres == iota((wide, inner), 1) // hdim).astype(F32)
    head_half = head_mask.astype(BF16)
    diagonal = (iota((nres, wide), 0) == iota((nres, wide), 1) % nres).astype(F32)
    lane_class = natural(iota((1, wide), 1) % nres) % n_head
    row_class = natural(iota((nres, 1), 0)) % n_head
    order = natural(iota((nres, nres), 0)) == iota((nres, nres), 1)
    key_row = (mask_ref[...].astype(F32) - 1.0) * MASKED
    key_bias = jnp.sum(jnp.where(order, key_row, 0.0), axis=1, keepdims=True)
    rows_of = iota((cells, cells), 0)
    cols_of = iota((cells, cells), 1)
    block = held * held
    pack = (
        rows_of % held * nres + rows_of // block * held + rows_of // held % held == cols_of
    ).astype(BF16)
    unpack = (
        rows_of // held % group * block + rows_of // nres * held + rows_of % held == cols_of
    ).astype(BF16)

    def expand(values):
        return jnp.concatenate([values] * heads, axis=0) * head_half

    def pick_heads(full):
        kept = full * head_mask
        total = kept[:nres]
        for h in range(1, heads):
            total = total + kept[h * nres : (h + 1) * nres]
        return total

    def flip_heads(values):
        turned = values.T
        return jnp.concatenate(
            [turned[h * nres : (h + 1) * nres] for h in range(heads)], axis=1
        )

    def wide_bias(which):
        rows = bias_ref[which].astype(F32)
        return jnp.concatenate(
            [jnp.broadcast_to(rows[h : h + 1], (nres, channels)) for h in range(heads)],
            axis=0,
        ).astype(BF16)

    def norm(values, which):
        return layer_norm(values, gain_ref[which : which + 1], shift_ref[which : which + 1])

    def split(values):
        return [values[r * nres : (r + 1) * nres] for r in range(held)]

    def bias_rows(normal, spread):
        full = mm(normal, spread, NT)
        rows = [jnp.sum(part * diagonal, axis=0, keepdims=True) for part in split(full)]
        return jnp.concatenate(rows, axis=0).astype(BF16).astype(F32)

    def project(normal, which):
        queries = (mm(normal, proj_ref[which, 0], NN) * scale).astype(BF16)
        keys = mm(normal, proj_ref[which, 1], NN).astype(BF16)
        values = mm(normal, proj_ref[which, 2], NN).astype(BF16)
        gate = jax.nn.sigmoid(
            mm(normal, proj_ref[which, 3], NN) + gate_ref[which : which + 1]
        )
        wide_queries = [expand(part) for part in split(queries)]
        key_parts = split(keys)
        logits = [mm(k, q, NT) + key_bias for k, q in zip(key_parts, wide_queries)]
        return key_parts, split(values), gate, wide_queries, logits

    def attend(parts, bias):
        keys, values, gate, wide_queries, logits = parts
        probs, halves, attended = [], [], []
        for r in range(held):
            scores = logits[r] + bias
            weights = jnp.exp(scores - jnp.max(scores, axis=0, keepdims=True))
            probs.append(weights / jnp.sum(weights, axis=0, keepdims=True))
            halves.append(probs[r].astype(BF16))
            attended.append(pick_heads(mm(halves[r], values[r], TN)))
        attended = jnp.concatenate(attended, axis=0)
        gated = (gate * attended).astype(BF16)
        return probs, halves, attended, gated

    def backward(parts, soft, grad_gated, which):
        keys, values, gate, wide_queries, unused = parts
        probs, halves, attended, gated = soft
        grad_att = split((grad_gated * gate).astype(BF16))
        grad_pre = (grad_gated * attended * gate * (1.0 - gate)).astype(BF16)
        picks = [(lane_class == c).astype(BF16) for c in range(n_head)]
        bias_sum, grad_queries = None, []
        grad_keys = [[] for c in range(n_head)]
        grad_values = [[] for c in range(n_head)]
        for r in range(held):
            wide_grads = expand(grad_att[r])
            grad_probs = mm(values[r], wide_grads, NT)
            grad_logits = probs[r] * (
                grad_probs - jnp.sum(probs[r] * grad_probs, axis=0, keepdims=True)
            )
            bias_sum = grad_logits if r == 0 else bias_sum + grad_logits
            logits_half = grad_logits.astype(BF16)
            grad_queries.append((pick_heads(mm(logits_half, keys[r], TN)) * scale).astype(BF16))
            by_key = mm(
                jnp.concatenate([logits_half * pick for pick in picks], axis=0),
                wide_queries[r],
                NN,
            ).astype(BF16)
            by_value = mm(
                jnp.concatenate([halves[r] * pick for pick in picks], axis=0), wide_grads, NN
            ).astype(BF16)
            for c in range(n_head):
                grad_keys[c].append(by_key[c * nres : (c + 1) * nres])
                grad_values[c].append(by_value[c * nres : (c + 1) * nres])
        grad_queries = jnp.concatenate(grad_queries, axis=0)
        grad_keys = [jnp.concatenate(part, axis=0) for part in grad_keys]
        grad_values = [jnp.concatenate(part, axis=0) for part in grad_values]
        query_side = mm(grad_queries, proj_ref[which, 0], NT) + mm(
            grad_pre, proj_ref[which, 3], NT
        )
        class_of = jnp.concatenate([row_class] * held, axis=0)
        partials = []
        for c in range(n_head):
            part = mm(grad_keys[c], proj_ref[which, 1], NT) + mm(
                grad_values[c], proj_ref[which, 2], NT
            )
            part = part + jnp.where(class_of == c, query_side, 0.0)
            partials.append(part.astype(BF16))
        return partials, bias_sum, (grad_queries, grad_keys, grad_values, grad_pre, gated)

    def stage_weights(normal, grads, grad_out, slot):
        grad_queries, grad_keys, grad_values, grad_pre, gated = grads
        repeated = jnp.concatenate([normal] * n_head, axis=0)
        matrices = [
            mm(normal, grad_queries, TN),
            mm(repeated, jnp.concatenate(grad_keys, axis=0), TN),
            mm(repeated, jnp.concatenate(grad_values, axis=0), TN),
            mm(normal, grad_pre, TN),
            mm(gated, grad_out, TN),
        ]
        tile = 0
        for matrix in matrices:
            half = matrix.astype(BF16)
            for r in range(matrix.shape[0] // TILE):
                stage_w[slot, tile % group, tile // group] = half[r * TILE : (r + 1) * TILE]
                tile += 1

    def bias_back(normal, spread, total):
        rounded = total.astype(BF16).astype(F32)
        placed = jnp.concatenate(
            [rounded[r : r + 1] * diagonal for r in range(held)], axis=0
        ).astype(BF16)
        grown = mm(placed, spread, NN)
        by_cell = mm(placed, normal, TN)
        rows = [
            jnp.sum(by_cell[h * nres : (h + 1) * nres], axis=0, keepdims=True)
            for h in range(heads)
        ]
        return grown, rows

    def stage_sums(which, rows, grad_pre, grad_normal, normed):
        rows = rows + [
            jnp.sum(grad_pre.astype(F32), axis=0, keepdims=True),
            jnp.sum(grad_normal * normed, axis=0, keepdims=True),
            jnp.sum(grad_normal, axis=0, keepdims=True),
        ]
        spare = stage_small.shape[1] - len(rows)
        if spare:
            rows = rows + [jnp.zeros((spare, channels), F32)]
        stage_small[which] = jnp.concatenate(rows, axis=0)

    def reduce_weights(slot):
        total = jnp.sum(got_w[slot].astype(F32), axis=0).astype(BF16)
        own_w[slot] = total
        all_w[slot, seat] = total

    order_half = order.astype(BF16)
    pair_own = mm(order_half, pair_ref[0], NN).astype(BF16)
    cot_own = mm(order_half, cot_ref[0], NN).astype(BF16)
    stage_in[0] = pair_own
    stage_in[1] = cot_own
    got_in[0, layer] = pair_own
    got_in[1, layer] = cot_own
    spread0 = wide_bias(0)
    spread1 = wide_bias(1)
    unused_normed, unused_inverse, normal_own = norm(pair_own, 0)
    row0 = jnp.sum(mm(normal_own, spread0, NT) * diagonal, axis=0, keepdims=True)
    row0 = row0.astype(BF16).astype(F32)
    stage_bias[...] = row0
    spot = seat * held + layer
    got_bias[spot] = row0
    pl.semaphore_wait(barrier, group * held - 1)
    send(lambda other: stage_bias, got_bias, 1, each_other, spot)
    send(lambda other: stage_in.at[0], got_in.at[0], 0, each_twin, layer)
    send(lambda other: stage_in.at[1], got_in.at[1], 12, each_twin, layer)
    for load in loads:
        load.wait()
    received(got_in.at[0], 0)
    first_in = got_in[0].reshape(cells, channels)

    normed0, inverse0, normal0 = norm(first_in, 0)
    parts0 = project(normal0, 0)
    received(got_in.at[1], 12)
    cotangent_half = got_in[1].reshape(cells, channels)
    cotangent = cotangent_half.astype(F32)
    packed_grad = mm(pack, cotangent_half, NN).astype(BF16)
    received(got_bias, 1)
    soft0 = attend(parts0, flip_heads(got_bias[...].reshape(nres, wide)))
    update = mm(soft0[3], out_ref[0], NN).astype(BF16)
    after_first = (first_in.astype(F32) + update.astype(F32)).astype(BF16)
    normed1, inverse1, normal1 = norm(after_first, 1)
    row1 = bias_rows(normal1, spread1)
    stage_bias1[...] = row1
    got_bias1[seat] = row1
    packed = mm(pack, after_first, NN).astype(BF16)
    packed = jnp.concatenate([packed, packed_grad], axis=1).reshape(group, block, 2 * channels)
    stage_flip[...] = packed
    got_flip[seat] = stage_flip[seat]
    send(lambda other: stage_flip.at[other], got_flip, 2)
    send(lambda other: stage_bias1, got_bias1, 3)
    received(got_flip, 2)

    flipped = mm(unpack, got_flip[...].reshape(cells, 2 * channels), NN).astype(BF16)
    column_grad = flipped[:, channels:]
    unused_normed, unused_inverse, normal_col = norm(flipped[:, :channels], 1)
    parts1 = project(normal_col, 1)
    grad_gated1 = mm(column_grad, out_ref[1], NT)
    received(got_bias1, 3)
    soft1 = attend(parts1, got_bias1[...].reshape(nres, wide))
    partials1, bias_sum1, grads1 = backward(parts1, soft1, grad_gated1, 1)
    stage_sum[1] = bias_sum1.reshape(group, held, wide)
    got_sum[1, seat] = stage_sum[1, seat]
    send(lambda other: stage_sum.at[1, other], got_sum.at[1], 4)
    back = mm(pack, jnp.concatenate(partials1, axis=1), NN).astype(BF16)
    stage_back[...] = back.reshape(group, block, n_head * channels)
    got_back[seat] = stage_back[seat]
    send(lambda other: stage_back.at[other], got_back, 5)
    stage_weights(normal_col, grads1, column_grad, 1)
    got_w[1, seat] = stage_w[1, seat]
    send(lambda other: stage_w.at[1, other], got_w.at[1], 6)
    received(got_sum.at[1], 4)
    grown1, rows1 = bias_back(normal1, spread1, jnp.sum(got_sum[1], axis=0))
    received(got_back, 5)
    back = mm(unpack, got_back[...].reshape(cells, n_head * channels), NN)
    grad_normal1 = back[:, :channels]
    for c in range(1, n_head):
        grad_normal1 = grad_normal1 + back[:, c * channels : (c + 1) * channels]
    grad_normal1 = grad_normal1 + grown1
    end_grad = norm_backward(grad_normal1, normed1, inverse1, gain_ref[1:2])
    grad_after = cotangent + end_grad.astype(BF16).astype(F32)
    grad_after_half = grad_after.astype(BF16)

    received(got_w.at[1], 6)
    reduce_weights(1)
    send(lambda other: own_w.at[1], all_w.at[1], 9)

    grad_gated0 = mm(grad_after_half, out_ref[0], NT)
    partials0, bias_sum0, grads0 = backward(parts0, soft0, grad_gated0, 0)
    stage_sum[0] = flip_heads(bias_sum0).reshape(group, held, wide)
    got_sum[0, seat] = stage_sum[0, seat]
    send(lambda other: stage_sum.at[0, other], got_sum.at[0], 7)
    stage_weights(normal0, grads0, grad_after_half, 0)
    got_w[0, seat] = stage_w[0, seat]
    send(lambda other: stage_w.at[0, other], got_w.at[0], 8)
    stage_sums(1, rows1, grads1[3], grad_normal1, normed1)
    received(got_sum.at[0], 7)
    grown0, rows0 = bias_back(normal0, spread0, jnp.sum(got_sum[0], axis=0))
    grad_normal0 = grown0
    for part in partials0:
        grad_normal0 = grad_normal0 + part.astype(F32)
    stage_sums(0, rows0, grads0[3], grad_normal0, normed0)
    got_small[seat] = stage_small[...]
    send(lambda other: stage_small, got_small, 10)
    start_grad = norm_backward(grad_normal0, normed0, inverse0, gain_ref[0:1])
    result[...] = (grad_after + start_grad).reshape(held, nres, channels)
    received(got_w.at[0], 8)
    reduce_weights(0)
    send(lambda other: own_w.at[0], all_w.at[0], 11)
    kept = result[layer]
    for p in range(nres):
        i = p % held * group + p // held
        pair_out[0, i : i + 1] = kept[p : p + 1]
    received(all_w.at[1], 9)
    weights_out[1] = all_w[1]
    received(got_small, 10)
    small_out[...] = jnp.sum(got_small[...], axis=0)
    received(all_w.at[0], 11)
    weights_out[0] = all_w[0]
    for target, channel in waits:
        wait_all(target, send_sem.at[channel])


def finish_kernel(
    heads,
    pair_in,
    weights_in,
    small_in,
    pair_out,
    proj_out,
    gate_out,
    outw_out,
    biasw_out,
    gain_out,
    shift_out,
):
    group = weights_in.shape[1]
    pair_out[...] = pair_in[...]
    for which in range(2):
        tile = 0
        for m in range(5):
            for r in range(proj_out.shape[2] // TILE):
                piece = weights_in[which, tile % group, tile // group].astype(F32)
                if m < 4:
                    proj_out[which, m, r * TILE : (r + 1) * TILE] = piece
                else:
                    outw_out[which, r * TILE : (r + 1) * TILE] = piece
                tile += 1
        small = small_in[which]
        biasw_out[which] = small[:heads]
        gate_out[which : which + 1] = small[heads : heads + 1]
        gain_out[which : which + 1] = small[heads + 1 : heads + 2]
        shift_out[which : which + 1] = small[heads + 2 : heads + 3]


def fused(
    row_count,
    head_count,
    pair_input,
    cotangent,
    residue_mask,
    norm_gain,
    norm_shift,
    proj_weights,
    gate_bias,
    out_weights,
    bias_weights,
):
    n = row_count * head_count
    held = RESIDENT
    group = n // held
    nres, channels = pair_input.shape[1:]
    heads = bias_weights.shape[2]
    slots = 5 * channels // TILE // group
    wide = heads * nres
    block = held * held
    small = -(-(heads + 3) // 8) * 8
    shape = jax.ShapeDtypeStruct
    vmem = pl.BlockSpec(memory_space=pltpu.VMEM)
    far = pl.BlockSpec(memory_space=pl.ANY)
    parts = pl.pallas_call(
        functools.partial(fused_kernel, head_count, held, group, heads),
        out_shape=(
            shape(pair_input.shape, F32),
            shape((2, group, slots, TILE, channels), BF16),
            shape((2, small, channels), F32),
        ),
        in_specs=[vmem] * 5 + [far, vmem, far, vmem],
        out_specs=[vmem] * 3,
        scratch_shapes=[
            pltpu.VMEM((2, nres, channels), BF16),
            pltpu.VMEM((2, held, nres, channels), BF16),
            pltpu.VMEM((1, wide), F32),
            pltpu.VMEM((n, 1, wide), F32),
            pltpu.VMEM((group, block, 2 * channels), BF16),
            pltpu.VMEM((group, block, 2 * channels), BF16),
            pltpu.VMEM((held, wide), F32),
            pltpu.VMEM((group, held, wide), F32),
            pltpu.VMEM((group, block, head_count * channels), BF16),
            pltpu.VMEM((group, block, head_count * channels), BF16),
            pltpu.VMEM((2, group, held, wide), F32),
            pltpu.VMEM((2, group, held, wide), F32),
            pltpu.VMEM((2, group, slots, TILE, channels), BF16),
            pltpu.VMEM((2, group, slots, TILE, channels), BF16),
            pltpu.VMEM((2, slots, TILE, channels), BF16),
            pltpu.VMEM((2, group, slots, TILE, channels), BF16),
            pltpu.VMEM((2, small, channels), F32),
            pltpu.VMEM((group, 2, small, channels), F32),
            pltpu.VMEM((held, nres, channels), F32),
            pltpu.VMEM(proj_weights.shape, BF16),
            pltpu.VMEM(out_weights.shape, BF16),
            pltpu.SemaphoreType.DMA((13,)),
            pltpu.SemaphoreType.DMA((13,)),
            pltpu.SemaphoreType.DMA((2,)),
        ],
        compiler_params=pltpu.CompilerParams(collective_id=0, has_side_effects=True),
    )(
        pair_input,
        cotangent,
        residue_mask.reshape(1, -1),
        norm_gain,
        norm_shift,
        proj_weights,
        gate_bias,
        out_weights,
        bias_weights.transpose(0, 2, 1),
    )
    outs = pl.pallas_call(
        functools.partial(finish_kernel, heads),
        out_shape=(
            shape(pair_input.shape, F32),
            shape(proj_weights.shape, F32),
            shape(gate_bias.shape, F32),
            shape(out_weights.shape, F32),
            shape((2, heads, channels), F32),
            shape(norm_gain.shape, F32),
            shape(norm_shift.shape, F32),
        ),
        in_specs=[vmem] * 3,
        out_specs=[vmem] * 7,
    )(*parts)
    outs = list(outs)
    outs[4] = outs[4].transpose(0, 2, 1)
    return tuple(outs)


def dispatch(row_count, head_count, *arrays):
    pair_input, proj_weights, bias_weights = arrays[0], arrays[5], arrays[8]
    rows, residues, channels = pair_input.shape
    inner = proj_weights.shape[3]
    wide = bias_weights.shape[2] * residues
    group = row_count * head_count // RESIDENT
    fits = (
        rows == 1
        and residues == group * RESIDENT
        and wide == inner == channels
        and 5 * channels % (TILE * group) == 0
    )
    if fits:
        return fused(row_count, head_count, *arrays)
    return local(*arrays)


def solution(mesh):
    return jax.shard_map(
        functools.partial(dispatch, mesh.shape["row"], mesh.shape["head"]),
        mesh=mesh,
        in_specs=(
            P(("row", "head"), None, None),
            P(("row", "head"), None, None),
            P(),
            P(),
            P(),
            P(),
            P(),
            P(),
            P(),
        ),
        out_specs=(P(("row", "head"), None, None), P(), P(), P(), P(), P(), P()),
        check_vma=False,
    )
```

profile of v0, /device:TPU:0, one launch (start us, length us, event | category | flops | bytes accessed | tf_op | source)
XLA Modules:
  0.0 35.9 jit_solution(9088575242112750729)
XLA Ops:
  0.6 33.5 %shard_map.144 = (f32[1,32,128]{2,1,0:T(8,128)}, bf16[2,8,5,16,128]{4,3,2,1,0:T(8,128)(2,1)}, f32[2,8,128]{2,1,0:T(8,128)}) custom-call(bf16[1,32,128]{2,1,0:T(8,128)(2,1)} %pair_ref.1, bf16[1,32,128]{2,1,0:T(8,128)(2,1)} %cot_ref.1, s32[1,32]{1,0:T(1,128)} %bitcast.4, f32[2,128]{1,0:T(2,128)} %gain_ref.1, f32[2,128]{1,0:T(2,128)} %shift_ref.1, ...), custom_call_target="tpu_custom_call" | custom-call | tf_op jit(solution)/shard_map/pallas_call | solution.py:816
  34.1 1.9 %shard_map.145 = (f32[1,32,128]{2,1,0:T(8,128)}, f32[2,4,128,128]{3,2,1,0:T(8,128)}, f32[2,128]{1,0:T(2,128)}, f32[2,128,128]{2,1,0:T(8,128)}, f32[2,4,128]{2,1,...) custom-call(f32[1,32,128]{2,1,0:T(8,128)} %get-tuple-element.17.pair_in, ...), custom_call_target="tpu_custom_call" | custom-call | tf_op jit(solution)/shard_map/pallas_call | solution.py:863
where the time goes:
time: 36.1 us; the launch traced here: 35.9 us
  Pallas kernels  35.3 us (98%)
  between operations  0.64 us (2%)
    pallas_call x1, Pallas kernels, fused(): pl.pallas_call(functools.partial(fused_kernel, head_count, held, group, h...  33.5 us
    pallas_call x1, Pallas kernels, fused(): pl.pallas_call(functools.partial(finish_kernel, heads), out_shape=(shape(...  1.85 us

commit v1 on v0

--- a/solution.py
+++ b/solution.py
@@ -342,6 +342,7 @@
 BF16 = jnp.bfloat16
 TILE = 16
 RESIDENT = 4
+VMEM_GRANT = 16 * 1024 * 1024
 NN = ((1,), (0,))
 NT = ((1,), (1,))
 TN = ((0,), (0,))
@@ -349,6 +350,10 @@
 
 def mm(a, b, contract):
     return lax.dot_general(a, b, (contract, ((), ())), preferred_element_type=F32)
+
+
+def bits_of(count):
+    return range(count.bit_length() - 1)
 
 
 def fused_kernel(
@@ -356,18 +361,27 @@
     held,
     group,
     heads,
+    pair_far,
+    cot_far,
+    mask_far,
+    gain_far,
+    shift_far,
+    proj_far,
+    gate_far,
+    out_far,
+    bias_far,
+    pair_out,
+    weights_out,
+    small_out,
     pair_ref,
     cot_ref,
     mask_ref,
     gain_ref,
     shift_ref,
-    proj_far,
+    proj_ref,
     gate_ref,
-    out_far,
+    out_ref,
     bias_ref,
-    pair_out,
-    weights_out,
-    small_out,
     stage_in,
     got_in,
     stage_bias,
@@ -383,23 +397,16 @@
     stage_w,
     got_w,
     own_w,
-    all_w,
     stage_small,
     got_small,
     result,
-    proj_ref,
-    out_ref,
     send_sem,
     recv_sem,
     load_sem,
 ):
-    loads = [
-        pltpu.make_async_copy(far, near, load_sem.at[i])
-        for i, (far, near) in enumerate(((proj_far, proj_ref), (out_far, out_ref)))
-    ]
-    for load in loads:
-        load.start()
-    me = lax.axis_index("row") * n_head + lax.axis_index("head")
+    row = lax.axis_index("row")
+    head = lax.axis_index("head")
+    me = row * n_head + head
     layer = me // group
     seat = me % group
     nres, channels = pair_ref.shape[1:]
@@ -411,60 +418,79 @@
     barrier = pltpu.get_barrier_semaphore()
     waits = []
 
-    def coords(device):
-        return (device // n_head, device % n_head)
-
-    def each_mate(action):
-        def step(offset, carry):
-            other = lax.rem(seat + offset, group)
-            action(other, coords(layer * group + other))
-            return carry
-
-        lax.fori_loop(1, group, step, 0)
-
-    def each_twin(action):
-        def step(offset, carry):
-            other = lax.rem(layer + offset, held)
-            action(other, coords(other * group + seat))
-            return carry
-
-        lax.fori_loop(1, held, step, 0)
-
-    def each_other(action):
-        def step(offset, carry):
-            other = lax.rem(me + offset, group * held)
-            action(other, coords(other))
-            return carry
-
-        lax.fori_loop(1, group * held, step, 0)
-
-    def send(source_of, target, channel, each=each_mate, slot=None):
+    seat_steps = []
+    for bit in bits_of(group):
+        step = 1 << bit
+        sign = 1 - 2 * (seat // step % 2)
+        if step < n_head:
+            seat_steps.append((sign * step, 0, sign * step))
+        else:
+            seat_steps.append((sign * step, sign * (step // n_head), 0))
+    layer_steps = []
+    for bit in bits_of(held):
+        step = 1 << bit
+        sign = 1 - 2 * (layer // step % 2)
+        layer_steps.append((sign * step, sign * (step * (group // n_head)), 0))
+
+    def partners(place, steps):
+        found = []
+        for flip in range((1 << len(steps)) - 1, 0, -1):
+            chosen = [steps[i] for i in range(len(steps)) if flip >> i & 1]
+            found.append(
+                (
+                    place + sum(part[0] for part in chosen),
+                    (row + sum(part[1] for part in chosen), head + sum(part[2] for part in chosen)),
+                )
+            )
+        return found
+
+    mates = partners(seat, seat_steps)
+    twins = partners(layer, layer_steps)
+
+    def send(source_of, target, channel, slot=None, peers=mates, part=None):
         place = seat if slot is None else slot
-
-        def start(other, device):
+        goal = target.at[place] if part is None else target.at[place, part]
+        for other, device in peers:
             pltpu.make_async_remote_copy(
                 src_ref=source_of(other),
-                dst_ref=target.at[place],
+                dst_ref=goal,
                 send_sem=send_sem.at[channel],
                 recv_sem=recv_sem.at[channel],
                 device_id=device,
                 device_id_type=MESH,
             ).start()
-
-        each(start)
-        waits.append((target, channel))
-
-    def wait_all(target, sem):
-        view = target.at[pl.ds(0, target.shape[0] - 1)]
+        waits.append((target, channel, part))
+
+    def wait_all(target, sem, part=None):
+        count = pl.ds(0, target.shape[0] - 1)
+        view = target.at[count] if part is None else target.at[count, part]
         pltpu.make_async_copy(view, view, sem).wait()
 
-    def received(target, channel):
-        wait_all(target, recv_sem.at[channel])
-
-    def greet(other, device):
+    def received(target, channel, part=None):
+        with jax.named_scope(f"w{channel}"):
+            wait_all(target, recv_sem.at[channel], part)
+
+    loads = {}
+    for i, (name, far, near) in enumerate(
+        (
+            ("pair", pair_far, pair_ref),
+            ("gain", gain_far, gain_ref),
+            ("shift", shift_far, shift_ref),
+            ("bias", bias_far, bias_ref),
+            ("cot", cot_far, cot_ref),
+            ("mask", mask_far, mask_ref),
+            ("proj", proj_far, proj_ref),
+            ("gate", gate_far, gate_ref),
+            ("out", out_far, out_ref),
+        )
+    ):
+        loads[name] = pltpu.make_async_copy(far, near, load_sem.at[i])
+    loads["pair"].start()
+    for other, device in twins + mates:
         pl.semaphore_signal(barrier, inc=1, device_id=device, device_id_type=MESH)
-
-    each_other(greet)
+    for name in loads:
+        if name != "pair":
+            loads[name].start()
 
     def iota(shape, dim):
         return lax.broadcasted_iota(jnp.int32, shape, dim)
@@ -475,11 +501,7 @@
     head_mask = (iota((wide, inner), 0) // nres == iota((wide, inner), 1) // hdim).astype(F32)
     head_half = head_mask.astype(BF16)
     diagonal = (iota((nres, wide), 0) == iota((nres, wide), 1) % nres).astype(F32)
-    lane_class = natural(iota((1, wide), 1) % nres) % n_head
-    row_class = natural(iota((nres, 1), 0)) % n_head
     order = natural(iota((nres, nres), 0)) == iota((nres, nres), 1)
-    key_row = (mask_ref[...].astype(F32) - 1.0) * MASKED
-    key_bias = jnp.sum(jnp.where(order, key_row, 0.0), axis=1, keepdims=True)
     rows_of = iota((cells, cells), 0)
     cols_of = iota((cells, cells), 1)
     block = held * held
@@ -549,67 +571,54 @@
         gated = (gate * attended).astype(BF16)
         return probs, halves, attended, gated
 
-    def backward(parts, soft, grad_gated, which):
+    def logit_grads(parts, soft, grad_gated):
         keys, values, gate, wide_queries, unused = parts
         probs, halves, attended, gated = soft
-        grad_att = split((grad_gated * gate).astype(BF16))
+        wide_grads = [expand(part) for part in split((grad_gated * gate).astype(BF16))]
         grad_pre = (grad_gated * attended * gate * (1.0 - gate)).astype(BF16)
-        picks = [(lane_class == c).astype(BF16) for c in range(n_head)]
-        bias_sum, grad_queries = None, []
-        grad_keys = [[] for c in range(n_head)]
-        grad_values = [[] for c in range(n_head)]
+        bias_sum, logit_halves = None, []
         for r in range(held):
-            wide_grads = expand(grad_att[r])
-            grad_probs = mm(values[r], wide_grads, NT)
+            grad_probs = mm(values[r], wide_grads[r], NT)
             grad_logits = probs[r] * (
                 grad_probs - jnp.sum(probs[r] * grad_probs, axis=0, keepdims=True)
             )
             bias_sum = grad_logits if r == 0 else bias_sum + grad_logits
-            logits_half = grad_logits.astype(BF16)
-            grad_queries.append((pick_heads(mm(logits_half, keys[r], TN)) * scale).astype(BF16))
-            by_key = mm(
-                jnp.concatenate([logits_half * pick for pick in picks], axis=0),
-                wide_queries[r],
-                NN,
-            ).astype(BF16)
-            by_value = mm(
-                jnp.concatenate([halves[r] * pick for pick in picks], axis=0), wide_grads, NN
-            ).astype(BF16)
-            for c in range(n_head):
-                grad_keys[c].append(by_key[c * nres : (c + 1) * nres])
-                grad_values[c].append(by_value[c * nres : (c + 1) * nres])
-        grad_queries = jnp.concatenate(grad_queries, axis=0)
-        grad_keys = [jnp.concatenate(part, axis=0) for part in grad_keys]
-        grad_values = [jnp.concatenate(part, axis=0) for part in grad_values]
-        query_side = mm(grad_queries, proj_ref[which, 0], NT) + mm(
-            grad_pre, proj_ref[which, 3], NT
+            logit_halves.append(grad_logits.astype(BF16))
+        return bias_sum, (wide_grads, grad_pre, logit_halves)
+
+    def cell_grads(parts, soft, found):
+        keys, values, gate, wide_queries, unused = parts
+        wide_grads, grad_pre, logit_halves = found
+        halves = soft[1]
+        queries_out, keys_out, values_out = [], [], []
+        for r in range(held):
+            queries_out.append((pick_heads(mm(logit_halves[r], keys[r], TN)) * scale).astype(BF16))
+            keys_out.append(mm(logit_halves[r], wide_queries[r], NN).astype(BF16))
+            values_out.append(mm(halves[r], wide_grads[r], NN).astype(BF16))
+        return (
+            jnp.concatenate(queries_out, axis=0),
+            jnp.concatenate(keys_out, axis=0),
+            jnp.concatenate(values_out, axis=0),
+            grad_pre,
         )
-        class_of = jnp.concatenate([row_class] * held, axis=0)
-        partials = []
-        for c in range(n_head):
-            part = mm(grad_keys[c], proj_ref[which, 1], NT) + mm(
-                grad_values[c], proj_ref[which, 2], NT
-            )
-            part = part + jnp.where(class_of == c, query_side, 0.0)
-            partials.append(part.astype(BF16))
-        return partials, bias_sum, (grad_queries, grad_keys, grad_values, grad_pre, gated)
-
-    def stage_weights(normal, grads, grad_out, slot):
-        grad_queries, grad_keys, grad_values, grad_pre, gated = grads
-        repeated = jnp.concatenate([normal] * n_head, axis=0)
-        matrices = [
-            mm(normal, grad_queries, TN),
-            mm(repeated, jnp.concatenate(grad_keys, axis=0), TN),
-            mm(repeated, jnp.concatenate(grad_values, axis=0), TN),
-            mm(normal, grad_pre, TN),
-            mm(gated, grad_out, TN),
-        ]
-        tile = 0
-        for matrix in matrices:
-            half = matrix.astype(BF16)
-            for r in range(matrix.shape[0] // TILE):
-                stage_w[slot, tile % group, tile // group] = half[r * TILE : (r + 1) * TILE]
-                tile += 1
+
+    def join(grads, which):
+        total = mm(grads[0], proj_ref[which, 0], NT)
+        for m in range(1, 4):
+            total = total + mm(grads[m], proj_ref[which, m], NT)
+        return total
+
+    def stage_matrix(slot, tile, matrix):
+        half = matrix.astype(BF16)
+        for r in range(matrix.shape[0] // TILE):
+            stage_w[slot, tile % group, tile // group] = half[r * TILE : (r + 1) * TILE]
+            tile += 1
+
+    def stage_weights(normal, grads, gated, grad_out, slot):
+        tiles = channels // TILE
+        for m in range(4):
+            stage_matrix(slot, m * tiles, mm(normal, grads[m], TN))
+        stage_matrix(slot, 4 * tiles, mm(gated, grad_out, TN))
 
     def bias_back(normal, spread, total):
         rounded = total.astype(BF16).astype(F32)
@@ -638,33 +647,35 @@
     def reduce_weights(slot):
         total = jnp.sum(got_w[slot].astype(F32), axis=0).astype(BF16)
         own_w[slot] = total
-        all_w[slot, seat] = total
+        weights_out[slot, seat] = total
 
     order_half = order.astype(BF16)
+    loads["pair"].wait()
     pair_own = mm(order_half, pair_ref[0], NN).astype(BF16)
+    stage_in[0] = pair_own
+    got_in[0, layer] = pair_own
+    loads["cot"].wait()
     cot_own = mm(order_half, cot_ref[0], NN).astype(BF16)
-    stage_in[0] = pair_own
     stage_in[1] = cot_own
-    got_in[0, layer] = pair_own
     got_in[1, layer] = cot_own
+    with jax.named_scope("bar"):
+        pl.semaphore_wait(barrier, len(twins) + len(mates))
+    send(lambda other: stage_in.at[0], got_in.at[0], 0, layer, twins)
+    send(lambda other: stage_in.at[1], got_in.at[1], 12, layer, twins)
+    for name in ("gain", "shift", "bias", "mask", "proj", "gate", "out"):
+        loads[name].wait()
+    key_row = (mask_ref[...].astype(F32) - 1.0) * MASKED
+    key_bias = jnp.sum(jnp.where(order, key_row, 0.0), axis=1, keepdims=True)
     spread0 = wide_bias(0)
     spread1 = wide_bias(1)
-    unused_normed, unused_inverse, normal_own = norm(pair_own, 0)
-    row0 = jnp.sum(mm(normal_own, spread0, NT) * diagonal, axis=0, keepdims=True)
-    row0 = row0.astype(BF16).astype(F32)
-    stage_bias[...] = row0
-    spot = seat * held + layer
-    got_bias[spot] = row0
-    pl.semaphore_wait(barrier, group * held - 1)
-    send(lambda other: stage_bias, got_bias, 1, each_other, spot)
-    send(lambda other: stage_in.at[0], got_in.at[0], 0, each_twin, layer)
-    send(lambda other: stage_in.at[1], got_in.at[1], 12, each_twin, layer)
-    for load in loads:
-        load.wait()
     received(got_in.at[0], 0)
     first_in = got_in[0].reshape(cells, channels)
-
     normed0, inverse0, normal0 = norm(first_in, 0)
+    row0 = bias_rows(normal0, spread0)
+    stage_bias[...] = row0
+    got_bias[seat] = row0
+    send(lambda other: stage_bias, got_bias, 1)
+
     parts0 = project(normal0, 0)
     received(got_in.at[1], 12)
     cotangent_half = got_in[1].reshape(cells, channels)
@@ -674,15 +685,15 @@
     soft0 = attend(parts0, flip_heads(got_bias[...].reshape(nres, wide)))
     update = mm(soft0[3], out_ref[0], NN).astype(BF16)
     after_first = (first_in.astype(F32) + update.astype(F32)).astype(BF16)
-    normed1, inverse1, normal1 = norm(after_first, 1)
-    row1 = bias_rows(normal1, spread1)
-    stage_bias1[...] = row1
-    got_bias1[seat] = row1
     packed = mm(pack, after_first, NN).astype(BF16)
     packed = jnp.concatenate([packed, packed_grad], axis=1).reshape(group, block, 2 * channels)
     stage_flip[...] = packed
     got_flip[seat] = stage_flip[seat]
     send(lambda other: stage_flip.at[other], got_flip, 2)
+    normed1, inverse1, normal1 = norm(after_first, 1)
+    row1 = bias_rows(normal1, spread1)
+    stage_bias1[...] = row1
+    got_bias1[seat] = row1
     send(lambda other: stage_bias1, got_bias1, 3)
     received(got_flip, 2)
 
@@ -693,47 +704,44 @@
     grad_gated1 = mm(column_grad, out_ref[1], NT)
     received(got_bias1, 3)
     soft1 = attend(parts1, got_bias1[...].reshape(nres, wide))
-    partials1, bias_sum1, grads1 = backward(parts1, soft1, grad_gated1, 1)
+    bias_sum1, found1 = logit_grads(parts1, soft1, grad_gated1)
     stage_sum[1] = bias_sum1.reshape(group, held, wide)
     got_sum[1, seat] = stage_sum[1, seat]
     send(lambda other: stage_sum.at[1, other], got_sum.at[1], 4)
-    back = mm(pack, jnp.concatenate(partials1, axis=1), NN).astype(BF16)
-    stage_back[...] = back.reshape(group, block, n_head * channels)
+    grads1 = cell_grads(parts1, soft1, found1)
+    back = mm(pack, join(grads1, 1).astype(BF16), NN).astype(BF16)
+    stage_back[...] = back.reshape(group, block, channels)
     got_back[seat] = stage_back[seat]
     send(lambda other: stage_back.at[other], got_back, 5)
-    stage_weights(normal_col, grads1, column_grad, 1)
+    stage_weights(normal_col, grads1, soft1[3], column_grad, 1)
     got_w[1, seat] = stage_w[1, seat]
     send(lambda other: stage_w.at[1, other], got_w.at[1], 6)
     received(got_sum.at[1], 4)
     grown1, rows1 = bias_back(normal1, spread1, jnp.sum(got_sum[1], axis=0))
     received(got_back, 5)
-    back = mm(unpack, got_back[...].reshape(cells, n_head * channels), NN)
-    grad_normal1 = back[:, :channels]
-    for c in range(1, n_head):
-        grad_normal1 = grad_normal1 + back[:, c * channels : (c + 1) * channels]
-    grad_normal1 = grad_normal1 + grown1
+    back = mm(unpack, got_back[...].reshape(cells, channels), NN)
+    grad_normal1 = back + grown1
     end_grad = norm_backward(grad_normal1, normed1, inverse1, gain_ref[1:2])
     grad_after = cotangent + end_grad.astype(BF16).astype(F32)
     grad_after_half = grad_after.astype(BF16)
 
-    received(got_w.at[1], 6)
-    reduce_weights(1)
-    send(lambda other: own_w.at[1], all_w.at[1], 9)
-
     grad_gated0 = mm(grad_after_half, out_ref[0], NT)
-    partials0, bias_sum0, grads0 = backward(parts0, soft0, grad_gated0, 0)
+    bias_sum0, found0 = logit_grads(parts0, soft0, grad_gated0)
     stage_sum[0] = flip_heads(bias_sum0).reshape(group, held, wide)
     got_sum[0, seat] = stage_sum[0, seat]
     send(lambda other: stage_sum.at[0, other], got_sum.at[0], 7)
-    stage_weights(normal0, grads0, grad_after_half, 0)
+    received(got_w.at[1], 6)
+    reduce_weights(1)
+    send(lambda other: own_w.at[1], weights_out.at[1], 9)
+    grads0 = cell_grads(parts0, soft0, found0)
+    stage_weights(normal0, grads0, soft0[3], grad_after_half, 0)
     got_w[0, seat] = stage_w[0, seat]
     send(lambda other: stage_w.at[0, other], got_w.at[0], 8)
     stage_sums(1, rows1, grads1[3], grad_normal1, normed1)
+    joined0 = join(grads0, 0)
     received(got_sum.at[0], 7)
     grown0, rows0 = bias_back(normal0, spread0, jnp.sum(got_sum[0], axis=0))
-    grad_normal0 = grown0
-    for part in partials0:
-        grad_normal0 = grad_normal0 + part.astype(F32)
+    grad_normal0 = grown0 + joined0
     stage_sums(0, rows0, grads0[3], grad_normal0, normed0)
     got_small[seat] = stage_small[...]
     send(lambda other: stage_small, got_small, 10)
@@ -741,19 +749,18 @@
     result[...] = (grad_after + start_grad).reshape(held, nres, channels)
     received(got_w.at[0], 8)
     reduce_weights(0)
-    send(lambda other: own_w.at[0], all_w.at[0], 11)
+    send(lambda other: own_w.at[0], weights_out.at[0], 11)
     kept = result[layer]
     for p in range(nres):
         i = p % held * group + p // held
         pair_out[0, i : i + 1] = kept[p : p + 1]
-    received(all_w.at[1], 9)
-    weights_out[1] = all_w[1]
+    received(weights_out.at[1], 9)
     received(got_small, 10)
     small_out[...] = jnp.sum(got_small[...], axis=0)
-    received(all_w.at[0], 11)
-    weights_out[0] = all_w[0]
-    for target, channel in waits:
-        wait_all(target, send_sem.at[channel])
+    received(weights_out.at[0], 11)
+    with jax.named_scope("ends"):
+        for target, channel, part in waits:
+            wait_all(target, send_sem.at[channel], part)
 
 
 def finish_kernel(
@@ -812,44 +819,8 @@
     small = -(-(heads + 3) // 8) * 8
     shape = jax.ShapeDtypeStruct
     vmem = pl.BlockSpec(memory_space=pltpu.VMEM)
-    far = pl.BlockSpec(memory_space=pl.ANY)
-    parts = pl.pallas_call(
-        functools.partial(fused_kernel, head_count, held, group, heads),
-        out_shape=(
-            shape(pair_input.shape, F32),
-            shape((2, group, slots, TILE, channels), BF16),
-            shape((2, small, channels), F32),
-        ),
-        in_specs=[vmem] * 5 + [far, vmem, far, vmem],
-        out_specs=[vmem] * 3,
-        scratch_shapes=[
-            pltpu.VMEM((2, nres, channels), BF16),
-            pltpu.VMEM((2, held, nres, channels), BF16),
-            pltpu.VMEM((1, wide), F32),
-            pltpu.VMEM((n, 1, wide), F32),
-            pltpu.VMEM((group, block, 2 * channels), BF16),
-            pltpu.VMEM((group, block, 2 * channels), BF16),
-            pltpu.VMEM((held, wide), F32),
-            pltpu.VMEM((group, held, wide), F32),
-            pltpu.VMEM((group, block, head_count * channels), BF16),
-            pltpu.VMEM((group, block, head_count * channels), BF16),
-            pltpu.VMEM((2, group, held, wide), F32),
-            pltpu.VMEM((2, group, held, wide), F32),
-            pltpu.VMEM((2, group, slots, TILE, channels), BF16),
-            pltpu.VMEM((2, group, slots, TILE, channels), BF16),
-            pltpu.VMEM((2, slots, TILE, channels), BF16),
-            pltpu.VMEM((2, group, slots, TILE, channels), BF16),
-            pltpu.VMEM((2, small, channels), F32),
-            pltpu.VMEM((group, 2, small, channels), F32),
-            pltpu.VMEM((held, nres, channels), F32),
-            pltpu.VMEM(proj_weights.shape, BF16),
-            pltpu.VMEM(out_weights.shape, BF16),
-            pltpu.SemaphoreType.DMA((13,)),
-            pltpu.SemaphoreType.DMA((13,)),
-            pltpu.SemaphoreType.DMA((2,)),
-        ],
-        compiler_params=pltpu.CompilerParams(collective_id=0, has_side_effects=True),
-    )(
+    far = pl.BlockSpec(memory_space=pltpu.HBM)
+    inputs = (
         pair_input,
         cotangent,
         residue_mask.reshape(1, -1),
@@ -860,6 +831,43 @@
         out_weights,
         bias_weights.transpose(0, 2, 1),
     )
+    parts = pl.pallas_call(
+        functools.partial(fused_kernel, head_count, held, group, heads),
+        out_shape=(
+            shape(pair_input.shape, F32),
+            shape((2, group, slots, TILE, channels), BF16),
+            shape((2, small, channels), F32),
+        ),
+        in_specs=[far] * len(inputs),
+        out_specs=[vmem] * 3,
+        scratch_shapes=[pltpu.VMEM(each.shape, each.dtype) for each in inputs]
+        + [
+            pltpu.VMEM((2, nres, channels), BF16),
+            pltpu.VMEM((2, held, nres, channels), BF16),
+            pltpu.VMEM((held, wide), F32),
+            pltpu.VMEM((group, held, wide), F32),
+            pltpu.VMEM((group, block, 2 * channels), BF16),
+            pltpu.VMEM((group, block, 2 * channels), BF16),
+            pltpu.VMEM((held, wide), F32),
+            pltpu.VMEM((group, held, wide), F32),
+            pltpu.VMEM((group, block, channels), BF16),
+            pltpu.VMEM((group, block, channels), BF16),
+            pltpu.VMEM((2, group, held, wide), F32),
+            pltpu.VMEM((2, group, held, wide), F32),
+            pltpu.VMEM((2, group, slots, TILE, channels), BF16),
+            pltpu.VMEM((2, group, slots, TILE, channels), BF16),
+            pltpu.VMEM((2, slots, TILE, channels), BF16),
+            pltpu.VMEM((2, small, channels), F32),
+            pltpu.VMEM((group, 2, small, channels), F32),
+            pltpu.VMEM((held, nres, channels), F32),
+            pltpu.SemaphoreType.DMA((13,)),
+            pltpu.SemaphoreType.DMA((13,)),
+            pltpu.SemaphoreType.DMA((len(inputs),)),
+        ],
+        compiler_params=pltpu.CompilerParams(
+            collective_id=0, has_side_effects=True, vmem_limit_bytes=VMEM_GRANT
+        ),
+    )(*(pltpu.with_memory_space_constraint(each, pltpu.HBM) for each in inputs))
     outs = pl.pallas_call(
         functools.partial(finish_kernel, heads),
         out_shape=(
@@ -873,6 +881,7 @@
         ),
         in_specs=[vmem] * 3,
         out_specs=[vmem] * 7,
+        compiler_params=pltpu.CompilerParams(vmem_limit_bytes=VMEM_GRANT),
     )(*parts)
     outs = list(outs)
     outs[4] = outs[4].transpose(0, 2, 1)
@@ -890,6 +899,8 @@
         and residues == group * RESIDENT
         and wide == inner == channels
         and 5 * channels % (TILE * group) == 0
+        and group & (group - 1) == 0
+        and group % head_count == 0
     )
     if fits:
         return fused(row_count, head_count, *arrays)

time: 36.1 us -> 33.5 us (0.928)
  Pallas kernels: 35.3 us -> 32.7 us
    pallas_call x1, Pallas kernels: 33.5 us -> 31.8 us  [fused(): pl.pallas_call(functools.partial(fused_kernel, head_count, held, group, h...]
    pallas_call x1, Pallas kernels: 1.85 us -> 0.88 us  [fused(): pl.pallas_call(functools.partial(finish_kernel, heads), out_shape=(shape(...]
where the time goes in v1:
time: 33.5 us; the launch traced here: 33.3 us
  Pallas kernels  32.7 us (98%)
  between operations  0.64 us (2%)
    pallas_call x1, Pallas kernels, fused(): pl.pallas_call(functools.partial(fused_kernel, head_count, held, group, h...  31.8 us
    pallas_call x1, Pallas kernels, fused(): pl.pallas_call(functools.partial(finish_kernel, heads), out_shape=(shape(...  0.88 us

profile of v1, /device:TPU:0, one launch (start us, length us, event | category | flops | bytes accessed | tf_op | source)
XLA Modules:
  0.0 33.3 jit_solution(8042306009117055039)
XLA Ops:
  0.6 31.8 %shard_map.144 = (f32[1,32,128]{2,1,0:T(8,128)S(1)}, bf16[2,8,5,16,128]{4,3,2,1,0:T(8,128)(2,1)S(1)}, f32[2,8,128]{2,1,0:T(8,128)S(1)}) custom-call(bf16[1,32,128]{2,1,0:T(8,128)(2,1)} %pair_far.1, bf16[1,32,128]{2,1,0:T(8,128)(2,1)} %cot_far.1, s32[1,32]{1,0:T(1,128)} %bitcast.4, f32[2,128]{1,0:T(2,128)} %gain_far.1, f32[2,128]{1,0:T(2,128)} %shift_far.1, ...), custom_call_target="tpu_custom_call" | custom-call | tf_op jit(solution)/shard_map/pallas_call | solution.py:834
  32.4 0.9 %shard_map.145 = (f32[1,32,128]{2,1,0:T(8,128)}, f32[2,4,128,128]{3,2,1,0:T(8,128)}, f32[2,128]{1,0:T(2,128)}, f32[2,128,128]{2,1,0:T(8,128)}, f32[2,4,128]{2,1,...) custom-call(f32[1,32,128]{2,1,0:T(8,128)S(1)} %get-tuple-element.17.pair_in, ...), custom_call_target="tpu_custom_call" | custom-call | tf_op jit(solution)/shard_map/pallas_call | solution.py:871

commit v2 on v1

--- a/solution.py
+++ b/solution.py
@@ -446,6 +446,7 @@
 
     mates = partners(seat, seat_steps)
     twins = partners(layer, layer_steps)
+    others = partners(0, seat_steps + layer_steps)
 
     def send(source_of, target, channel, slot=None, peers=mates, part=None):
         place = seat if slot is None else slot
@@ -486,7 +487,7 @@
     ):
         loads[name] = pltpu.make_async_copy(far, near, load_sem.at[i])
     loads["pair"].start()
-    for other, device in twins + mates:
+    for other, device in others:
         pl.semaphore_signal(barrier, inc=1, device_id=device, device_id_type=MESH)
     for name in loads:
         if name != "pair":
@@ -586,21 +587,17 @@
             logit_halves.append(grad_logits.astype(BF16))
         return bias_sum, (wide_grads, grad_pre, logit_halves)
 
-    def cell_grads(parts, soft, found):
+    def value_grads(soft, wide_grads):
+        parts = [mm(half, wide, NN).astype(BF16) for half, wide in zip(soft[1], wide_grads)]
+        return jnp.concatenate(parts, axis=0)
+
+    def query_key_grads(parts, logit_halves):
         keys, values, gate, wide_queries, unused = parts
-        wide_grads, grad_pre, logit_halves = found
-        halves = soft[1]
-        queries_out, keys_out, values_out = [], [], []
+        queries_out, keys_out = [], []
         for r in range(held):
             queries_out.append((pick_heads(mm(logit_halves[r], keys[r], TN)) * scale).astype(BF16))
             keys_out.append(mm(logit_halves[r], wide_queries[r], NN).astype(BF16))
-            values_out.append(mm(halves[r], wide_grads[r], NN).astype(BF16))
-        return (
-            jnp.concatenate(queries_out, axis=0),
-            jnp.concatenate(keys_out, axis=0),
-            jnp.concatenate(values_out, axis=0),
-            grad_pre,
-        )
+        return [jnp.concatenate(queries_out, axis=0), jnp.concatenate(keys_out, axis=0)]
 
     def join(grads, which):
         total = mm(grads[0], proj_ref[which, 0], NT)
@@ -614,11 +611,18 @@
             stage_w[slot, tile % group, tile // group] = half[r * TILE : (r + 1) * TILE]
             tile += 1
 
-    def stage_weights(normal, grads, gated, grad_out, slot):
-        tiles = channels // TILE
-        for m in range(4):
-            stage_matrix(slot, m * tiles, mm(normal, grads[m], TN))
-        stage_matrix(slot, 4 * tiles, mm(gated, grad_out, TN))
+    tiles = channels // TILE
+    early = pl.ds(0, 3 * tiles // group)
+    late = pl.ds(3 * tiles // group, 2 * tiles // group)
+
+    def stage_early(normal, grads, gated, grad_out, slot):
+        stage_matrix(slot, 0, mm(gated, grad_out, TN))
+        stage_matrix(slot, tiles, mm(normal, grads[3], TN))
+        stage_matrix(slot, 2 * tiles, mm(normal, grads[2], TN))
+
+    def stage_late(normal, grads, slot):
+        stage_matrix(slot, 3 * tiles, mm(normal, grads[0], TN))
+        stage_matrix(slot, 4 * tiles, mm(normal, grads[1], TN))
 
     def bias_back(normal, spread, total):
         rounded = total.astype(BF16).astype(F32)
@@ -642,39 +646,54 @@
         spare = stage_small.shape[1] - len(rows)
         if spare:
             rows = rows + [jnp.zeros((spare, channels), F32)]
-        stage_small[which] = jnp.concatenate(rows, axis=0)
-
-    def reduce_weights(slot):
-        total = jnp.sum(got_w[slot].astype(F32), axis=0).astype(BF16)
-        own_w[slot] = total
-        weights_out[slot, seat] = total
+        rows = jnp.concatenate(rows, axis=0)
+        stage_small[which] = rows
+        got_small[which, seat] = rows
+
+    def send_weights(slot, part, channel):
+        got_w[slot, seat, part] = stage_w[slot, seat, part]
+        send(lambda other: stage_w.at[slot, other, part], got_w.at[slot], channel, part=part)
+
+    def pass_weights(slot, part, channel, next_channel):
+        received(got_w.at[slot], channel, part)
+        total = jnp.sum(got_w[slot, :, part].astype(F32), axis=0).astype(BF16)
+        own_w[slot, part] = total
+        weights_out[slot, seat, part] = total
+        send(
+            lambda other: own_w.at[slot, part], weights_out.at[slot], next_channel, part=part
+        )
 
     order_half = order.astype(BF16)
     loads["pair"].wait()
     pair_own = mm(order_half, pair_ref[0], NN).astype(BF16)
     stage_in[0] = pair_own
     got_in[0, layer] = pair_own
+    for name in ("gain", "shift", "bias"):
+        loads[name].wait()
+    spread0 = wide_bias(0)
+    unused_normed, unused_inverse, normal_own = norm(pair_own, 0)
+    row0 = jnp.sum(mm(normal_own, spread0, NT) * diagonal, axis=0, keepdims=True)
+    row0 = row0.astype(BF16).astype(F32)
+    stage_bias[...] = row0
+    spot = seat * held + layer
+    got_bias[spot] = row0
     loads["cot"].wait()
     cot_own = mm(order_half, cot_ref[0], NN).astype(BF16)
     stage_in[1] = cot_own
     got_in[1, layer] = cot_own
     with jax.named_scope("bar"):
-        pl.semaphore_wait(barrier, len(twins) + len(mates))
+        pl.semaphore_wait(barrier, len(others))
     send(lambda other: stage_in.at[0], got_in.at[0], 0, layer, twins)
+    send(lambda other: stage_bias, got_bias, 1, spot, others)
     send(lambda other: stage_in.at[1], got_in.at[1], 12, layer, twins)
-    for name in ("gain", "shift", "bias", "mask", "proj", "gate", "out"):
+    for name in ("mask", "proj", "gate", "out"):
         loads[name].wait()
     key_row = (mask_ref[...].astype(F32) - 1.0) * MASKED
     key_bias = jnp.sum(jnp.where(order, key_row, 0.0), axis=1, keepdims=True)
-    spread0 = wide_bias(0)
     spread1 = wide_bias(1)
     received(got_in.at[0], 0)
     first_in = got_in[0].reshape(cells, channels)
     normed0, inverse0, normal0 = norm(first_in, 0)
-    row0 = bias_rows(normal0, spread0)
-    stage_bias[...] = row0
-    got_bias[seat] = row0
-    send(lambda other: stage_bias, got_bias, 1)
 
     parts0 = project(normal0, 0)
     received(got_in.at[1], 12)
@@ -708,14 +727,16 @@
     stage_sum[1] = bias_sum1.reshape(group, held, wide)
     got_sum[1, seat] = stage_sum[1, seat]
     send(lambda other: stage_sum.at[1, other], got_sum.at[1], 4)
-    grads1 = cell_grads(parts1, soft1, found1)
+    grads1 = query_key_grads(parts1, found1[2])
+    grads1 = grads1 + [value_grads(soft1, found1[0]), found1[1]]
     back = mm(pack, join(grads1, 1).astype(BF16), NN).astype(BF16)
     stage_back[...] = back.reshape(group, block, channels)
     got_back[seat] = stage_back[seat]
     send(lambda other: stage_back.at[other], got_back, 5)
-    stage_weights(normal_col, grads1, soft1[3], column_grad, 1)
-    got_w[1, seat] = stage_w[1, seat]
-    send(lambda other: stage_w.at[1, other], got_w.at[1], 6)
+    stage_early(normal_col, grads1, soft1[3], column_grad, 1)
+    stage_late(normal_col, grads1, 1)
+    every = pl.ds(0, 5 * tiles // group)
+    send_weights(1, every, 6)
     received(got_sum.at[1], 4)
     grown1, rows1 = bias_back(normal1, spread1, jnp.sum(got_sum[1], axis=0))
     received(got_back, 5)
@@ -729,35 +750,37 @@
     bias_sum0, found0 = logit_grads(parts0, soft0, grad_gated0)
     stage_sum[0] = flip_heads(bias_sum0).reshape(group, held, wide)
     got_sum[0, seat] = stage_sum[0, seat]
+    value0 = value_grads(soft0, found0[0])
+    stage_early(normal0, [None, None, value0, found0[1]], soft0[3], grad_after_half, 0)
     send(lambda other: stage_sum.at[0, other], got_sum.at[0], 7)
-    received(got_w.at[1], 6)
-    reduce_weights(1)
-    send(lambda other: own_w.at[1], weights_out.at[1], 9)
-    grads0 = cell_grads(parts0, soft0, found0)
-    stage_weights(normal0, grads0, soft0[3], grad_after_half, 0)
-    got_w[0, seat] = stage_w[0, seat]
-    send(lambda other: stage_w.at[0, other], got_w.at[0], 8)
+    send_weights(0, early, 8)
+    grads0 = query_key_grads(parts0, found0[2]) + [value0, found0[1]]
+    stage_late(normal0, grads0, 0)
+    send_weights(0, late, 14)
     stage_sums(1, rows1, grads1[3], grad_normal1, normed1)
+    send(lambda other: stage_small.at[1], got_small.at[1], 13)
+    pass_weights(1, every, 6, 9)
     joined0 = join(grads0, 0)
     received(got_sum.at[0], 7)
     grown0, rows0 = bias_back(normal0, spread0, jnp.sum(got_sum[0], axis=0))
     grad_normal0 = grown0 + joined0
     stage_sums(0, rows0, grads0[3], grad_normal0, normed0)
-    got_small[seat] = stage_small[...]
-    send(lambda other: stage_small, got_small, 10)
+    send(lambda other: stage_small.at[0], got_small.at[0], 10)
+    pass_weights(0, early, 8, 11)
+    pass_weights(0, late, 14, 15)
     start_grad = norm_backward(grad_normal0, normed0, inverse0, gain_ref[0:1])
     result[...] = (grad_after + start_grad).reshape(held, nres, channels)
-    received(got_w.at[0], 8)
-    reduce_weights(0)
-    send(lambda other: own_w.at[0], weights_out.at[0], 11)
     kept = result[layer]
     for p in range(nres):
         i = p % held * group + p // held
         pair_out[0, i : i + 1] = kept[p : p + 1]
-    received(weights_out.at[1], 9)
-    received(got_small, 10)
-    small_out[...] = jnp.sum(got_small[...], axis=0)
-    received(weights_out.at[0], 11)
+    received(got_small.at[1], 13)
+    small_out[1] = jnp.sum(got_small[1], axis=0)
+    received(weights_out.at[1], 9, every)
+    received(got_small.at[0], 10)
+    small_out[0] = jnp.sum(got_small[0], axis=0)
+    received(weights_out.at[0], 11, early)
+    received(weights_out.at[0], 15, late)
     with jax.named_scope("ends"):
         for target, channel, part in waits:
             wait_all(target, send_sem.at[channel], part)
@@ -780,7 +803,7 @@
     pair_out[...] = pair_in[...]
     for which in range(2):
         tile = 0
-        for m in range(5):
+        for m in (4, 3, 2, 0, 1):
             for r in range(proj_out.shape[2] // TILE):
                 piece = weights_in[which, tile % group, tile // group].astype(F32)
                 if m < 4:
@@ -844,8 +867,8 @@
         + [
             pltpu.VMEM((2, nres, channels), BF16),
             pltpu.VMEM((2, held, nres, channels), BF16),
-            pltpu.VMEM((held, wide), F32),
-            pltpu.VMEM((group, held, wide), F32),
+            pltpu.VMEM((1, wide), F32),
+            pltpu.VMEM((n, 1, wide), F32),
             pltpu.VMEM((group, block, 2 * channels), BF16),
             pltpu.VMEM((group, block, 2 * channels), BF16),
             pltpu.VMEM((held, wide), F32),
@@ -858,10 +881,10 @@
             pltpu.VMEM((2, group, slots, TILE, channels), BF16),
             pltpu.VMEM((2, slots, TILE, channels), BF16),
             pltpu.VMEM((2, small, channels), F32),
-            pltpu.VMEM((group, 2, small, channels), F32),
+            pltpu.VMEM((2, group, small, channels), F32),
             pltpu.VMEM((held, nres, channels), F32),
-            pltpu.SemaphoreType.DMA((13,)),
-            pltpu.SemaphoreType.DMA((13,)),
+            pltpu.SemaphoreType.DMA((16,)),
+            pltpu.SemaphoreType.DMA((16,)),
             pltpu.SemaphoreType.DMA((len(inputs),)),
         ],
         compiler_params=pltpu.CompilerParams(
@@ -898,7 +921,7 @@
         rows == 1
         and residues == group * RESIDENT
         and wide == inner == channels
-        and 5 * channels % (TILE * group) == 0
+        and channels % (TILE * group) == 0
         and group & (group - 1) == 0
         and group % head_count == 0
     )

time: 33.5 us -> 30.6 us (0.913)
  Pallas kernels: 32.7 us -> 29.7 us
    pallas_call x1, Pallas kernels: 31.8 us -> 28.9 us  [fused(): pl.pallas_call(functools.partial(fused_kernel, head_count, held, group, h...]
where the time goes in v2:
time: 30.6 us; the launch traced here: 30.4 us
  Pallas kernels  29.7 us (97%)
  between operations  0.64 us (2%)
    pallas_call x1, Pallas kernels, fused(): pl.pallas_call(functools.partial(fused_kernel, head_count, held, group, h...  28.9 us
    pallas_call x1, Pallas kernels, fused(): pl.pallas_call(functools.partial(finish_kernel, heads), out_shape=(shape(...  0.89 us

profile of v2, /device:TPU:0, one launch (start us, length us, event | category | flops | bytes accessed | tf_op | source)
XLA Modules:
  0.0 30.4 jit_solution(17784519572671941359)
XLA Ops:
  0.6 28.9 %shard_map.144 = (f32[1,32,128]{2,1,0:T(8,128)S(1)}, bf16[2,8,5,16,128]{4,3,2,1,0:T(8,128)(2,1)S(1)}, f32[2,8,128]{2,1,0:T(8,128)S(1)}) custom-call(bf16[1,32,128]{2,1,0:T(8,128)(2,1)} %pair_far.1, bf16[1,32,128]{2,1,0:T(8,128)(2,1)} %cot_far.1, s32[1,32]{1,0:T(1,128)} %bitcast.4, f32[2,128]{1,0:T(2,128)} %gain_far.1, f32[2,128]{1,0:T(2,128)} %shift_far.1, ...), custom_call_target="tpu_custom_call" | custom-call | tf_op jit(solution)/shard_map/pallas_call | solution.py:857
  29.5 0.9 %shard_map.145 = (f32[1,32,128]{2,1,0:T(8,128)}, f32[2,4,128,128]{3,2,1,0:T(8,128)}, f32[2,128]{1,0:T(2,128)}, f32[2,128,128]{2,1,0:T(8,128)}, f32[2,4,128]{2,1,...) custom-call(f32[1,32,128]{2,1,0:T(8,128)S(1)} %get-tuple-element.17.pair_in, ...), custom_call_target="tpu_custom_call" | custom-call | tf_op jit(solution)/shard_map/pallas_call | solution.py:894
